TPU v7x, 128 devices: a whole 4x4x4 slice. The times are simulated.
128 devices in a mesh: member: 2 (over core), grid: 64 (over z, y, x).
Axes of the slice: x: 4, y: 4, z: 4, core: 2. Of those that a mesh axis runs over, the one named last changes fastest.
Arguments:
- latent: bfloat16 [4, 131072, 512], P('member', 'grid'), may hold values from -80 to 80
- block_pick: int32 [64, 64], P('grid'), may hold values from 0 to 15
- obs_weight: bfloat16 [64, 64, 32, 128], P('grid'), may hold values from 0.0099487305 to 1
- obs_value: float32 [64, 64, 32, 128], P('grid'), may hold values from -6 to 6
- obs_count: int32 [64, 64], P('grid'), may hold values from 0 to 32, as said below
- w_in: bfloat16 [512, 512], replicated, may hold values from -0.25 to 0.25
- b_in: float32 [512], replicated, may hold values from -3 to 3
- w_out: bfloat16 [512, 128], replicated, may hold values from -0.25 to 0.25
- b_out: float32 [128], replicated, may hold values from -3 to 3
Outputs:
- latent_grad: float32 [4, 131072, 512], P('member', 'grid')
- loss_value: float32 [], replicated
Inputs may be any that keep to these rules, and one draw needn't show every extreme that they name: Entry [d, j] counts the live observations of those slots; the live ones are the first slots, k < obs_count[d, j].
All inputs are finite; a program needn't handle non-finite values.
Results may differ from a plain program's by a relative error of at most 0.0041.
Values may be sent and summed in bfloat16 or wider, within the bound.
No kernel may reach another device: no remote copies, remote signals or barrier semaphores. Data moves between devices by JAX's collectives and lax.ppermute only.
A program may use at most 128 MiB of HBM per device.

v0:
```python
import jax
import jax.numpy as jnp
from jax import lax
from jax.sharding import Mesh
from jax.sharding import PartitionSpec as P

GRID = ("grid_0", "grid_1", "grid_2")
MEMBER_GRID = ("member", "grid_0", "grid_1", "grid_2")
SOFTEN = 0.1


def sent_to_all(value, axis):
    copies = jnp.broadcast_to(value, (lax.axis_size(axis), *value.shape))
    return lax.all_to_all(copies, axis, split_axis=0, concat_axis=0, tiled=True)


def taken_together(value, axis):
    everything = sent_to_all(value, axis)
    return jnp.sum(everything, axis=0)


def one_axis_at_a_time(value, axes):
    for axis in axes:
        value = lax.psum(value, axis)
    return value


def smooth_abs(value):
    return jnp.sqrt(value * value + SOFTEN * SOFTEN)


def silu_slope(pre_act):
    sigmoid_value = jax.nn.sigmoid(pre_act)
    return sigmoid_value * (1.0 + pre_act * (1.0 - sigmoid_value))


def per_device(latent, block_pick, obs_weight, obs_value, obs_count, w_in, b_in, w_out, b_out):
    members_here, points, feature_width = latent.shape
    peer_count = lax.axis_size(GRID)
    slot_count = obs_weight.shape[2]
    block_size = obs_weight.shape[3]
    channels = obs_value.shape[3]
    members_all = members_here * lax.axis_size("member")
    block_count = points // block_size
    local_blocks = latent.reshape(members_here, block_count, block_size, feature_width)
    picked_ids = block_pick[0]
    block_onehot = (
        picked_ids[:, None] == jnp.arange(block_count, dtype=jnp.int32)[None, :]
    ).astype(jnp.bfloat16)
    weight_sum = jnp.sum(obs_weight[0], axis=2, keepdims=True, dtype=jnp.float32)
    norm_weight = (obs_weight[0] / weight_sum).astype(jnp.bfloat16)
    picked = local_blocks[:, picked_ids]
    owner_weight = lax.all_to_all(norm_weight, GRID, split_axis=0, concat_axis=0, tiled=True)
    owner_interp = jnp.einsum(
        "dkp,mdpc->mdkc", owner_weight, picked, preferred_element_type=jnp.float32
    ).astype(jnp.bfloat16)
    interp = lax.all_to_all(owner_interp, GRID, split_axis=1, concat_axis=1, tiled=True)
    flat_rows = interp.reshape(members_here * peer_count * slot_count, feature_width)
    pre_act = jnp.dot(flat_rows, w_in, preferred_element_type=jnp.float32) + b_in
    hidden = jax.nn.silu(pre_act).astype(jnp.bfloat16)
    predicted = jnp.dot(hidden, w_out, preferred_element_type=jnp.float32) + b_out
    predicted = predicted.reshape(members_here, peer_count, slot_count, channels)
    all_members = lax.all_gather(predicted, "member", axis=0, tiled=True)
    target = obs_value[0]
    live_mask = (jnp.arange(slot_count, dtype=jnp.int32)[None, :] < obs_count[0][:, None]).astype(
        jnp.float32
    )
    obs_diff = predicted - target[None]
    pair_diff = predicted[:, None] - all_members[None]
    per_obs = smooth_abs(obs_diff) / members_all - jnp.sum(smooth_abs(pair_diff), axis=1) / (
        2.0 * members_all * (members_all - 1)
    )
    loss_part = jnp.sum(per_obs * live_mask[None, :, :, None])
    live_count = jnp.sum(live_mask)
    live_total = taken_together(live_count, GRID)
    loss_total = one_axis_at_a_time(loss_part, MEMBER_GRID)
    loss_value = loss_total / (channels * live_total)
    grad_scale = peer_count * peer_count * slot_count / live_total
    slope_obs = obs_diff / smooth_abs(obs_diff)
    slope_pair = jnp.sum(pair_diff / smooth_abs(pair_diff), axis=1)
    grad_pred = (
        grad_scale
        * live_mask[None, :, :, None]
        * (slope_obs / members_all - slope_pair / (members_all * (members_all - 1.0)))
    ).astype(jnp.bfloat16)
    grad_hidden = jnp.einsum(
        "rv,hv->rh", grad_pred.reshape(-1, channels), w_out, preferred_element_type=jnp.float32
    )
    grad_act = (grad_hidden * silu_slope(pre_act)).astype(jnp.bfloat16)
    grad_interp = jnp.einsum(
        "rh,ch->rc", grad_act, w_in, preferred_element_type=jnp.float32
    ).astype(jnp.bfloat16)
    grad_interp = grad_interp.reshape(members_here, peer_count, slot_count, feature_width)
    owner_grad = lax.all_to_all(grad_interp, GRID, split_axis=1, concat_axis=1, tiled=True)
    returned = jnp.einsum(
        "dkp,mdkc->mdpc", owner_weight, owner_grad, preferred_element_type=jnp.float32
    ).astype(jnp.bfloat16)
    summed = jnp.einsum("mdpc,db->mbpc", returned, block_onehot, preferred_element_type=jnp.float32)
    latent_grad = summed.reshape(members_here, points, feature_width)
    return (latent_grad, loss_value)


def solution(mesh):
    split = Mesh(
        mesh.devices.reshape(mesh.shape["member"], 4, 4, 4),
        ("member", "grid_0", "grid_1", "grid_2"),
    )
    return jax.shard_map(
        per_device,
        mesh=split,
        in_specs=(
            P("member", GRID, None),
            P(GRID, None),
            P(GRID, None, None, None),
            P(GRID, None, None, None),
            P(GRID, None),
            P(),
            P(),
            P(),
            P(),
        ),
        out_specs=(P("member", GRID, None), P()),
        check_vma=False,
    )
```

profile of v0, /device:TPU:0, one launch (start us, length us, event | category | flops | bytes accessed | tf_op | source)
XLA Modules:
  0.0 289.0 jit_solution(11307042710669002750)
XLA Ops:
  7.2 1.4 convert_reduce_fusion
  8.6 2.2 fusion.13
  10.8 11.5 %all-to-all-start.1 = ((bf16[64,32,128]{2,1,0:T(8,128)(2,1)}), bf16[64,32,128]{2,1,0:T(8,128)(2,1)S(1)}, u32[]{:S(2)}, u32[]{:S(2)}) async-start(bf16[64,32,128]{2,1,0:T(8,128)(2,1)} %fusion.13), calls=%async_computation.1 | async-start | bytes 1048576 | tf_op jit(solution)/shard_map/all_to_all | solution.py:53
  22.4 0.7 fusion.22
  23.1 9.7 %gather_fusion = bf16[64,2,128,512]{3,2,1,0:T(8,128)(2,1)} fusion(bf16[2,16,128,512]{3,2,1,0:T(8,128)(2,1)} %bitcast.67, s32[1024]{0:T(1024)S(1)} %pad_clamp_fusion), kind=kCustom, calls=%fused_computation | custom fusion | bytes 33554688 | tf_op jit(solution)/shard_map/gather | solution.py:52
  32.8 2.9 %all-to-all-done.1 = bf16[64,32,128]{2,1,0:T(8,128)(2,1)S(1)} async-done(((bf16[64,32,128]{2,1,0:T(8,128)(2,1)}), bf16[64,32,128]{2,1,0:T(8,128)(2,1)S(1)}, u32[]{:S(2)}, u32[]{:S(2)}) %all-to-all-start.1) | async-done | bytes 524320 | tf_op jit(solution)/shard_map/all_to_all | solution.py:53
  35.7 8.1 %convert_bitcast_fusion.1 = bf16[2,64,32,512]{3,2,0,1:T(8,128)(2,1)S(1)} fusion(bf16[64,2,128,512]{3,2,1,0:T(8,128)(2,1)} %gather_fusion, bf16[64,32,128]{2,1,0:T(8,128)(2,1)S(1)} %all-to-all-done.1), kind=kOutput, calls=%fused_computation.15 | convolution fusion | flops 538968064 | bytes 21495808 | tf_op jit(solution)/shard_map/dkp,mdpc->mdkc/dot_general | solution.py:54
  43.8 59.1 %all_to_all.21 = bf16[2,64,32,512]{3,2,0,1:T(8,128)(2,1)S(1)} all-to-all(bf16[2,64,32,512]{3,2,0,1:T(8,128)(2,1)S(1)} %convert_bitcast_fusion.1), channel_id=1, replica_groups=mesh['member'=2,'grid_0'=4,'grid_1'=4,'grid_2'=4] {'grid_0','grid_1','gr..., dimensions={1} | all-to-all | bytes 8388608 | tf_op jit(solution)/shard_map/all_to_all | solution.py:57
  102.9 0.6 copy.22
  103.6 2.4 fusion.25
  106.1 4.1 %convolution_add_fusion = f32[4096,128]{1,0:T(8,128)} fusion(bf16[512,128]{1,0:T(8,128)(2,1)S(1)} %copy-done.7, f32[4096,512]{1,0:T(8,128)S(1)} %fusion.25, f32[512]{0:T(512)S(1)} %copy-done.8, f32[128]{0:T(128)S(1)} %copy-done.9), kind=kOutput, calls=%fused_computation.14 | convolution fusion | flops 549978112 | bytes 10619392 | tf_op jit(solution)/shard_map/dot_general | solution.py:61
  110.2 0.7 fusion.18
  110.8 1.3 broadcast_in_dim.2
  112.1 6.0 %all-to-all-start = ((f32[64,1,1]{2,1,0:T(1,128)}), f32[64,1,1]{2,1,0:T(1,128)S(1)}, u32[]{:S(2)}, u32[]{:S(2)}) async-start(f32[64,1,1]{2,1,0:T(1,128)} %broadcast_in_dim.2), calls=%async_computation | async-start | bytes 65536 | tf_op jit(solution)/shard_map/all_to_all | solution.py:14
  118.3 9.2 %all-to-all-done = f32[64,1,1]{2,1,0:T(1,128)S(1)} async-done(((f32[64,1,1]{2,1,0:T(1,128)}), f32[64,1,1]{2,1,0:T(1,128)S(1)}, u32[]{:S(2)}, u32[]{:S(2)}) %all-to-all-start) | async-done | bytes 288 | tf_op jit(solution)/shard_map/all_to_all | solution.py:14
  127.5 0.7 reduce_sum.55
  129.1 7.4 %fusion.4 = (f32[2,64,32,128]{3,2,1,0:T(8,128)S(1)}, f32[2,64,32,128]{3,2,1,0:T(8,128)S(1)}) fusion(f32[4,64,32,128]{3,2,1,0:T(8,128)} %all-gather.2.cloned.1.call-done, f32[2,64,32,128]{3,2,1,0:T(8,128)} %bitcast.69), kind=kLoop, calls=%fused_computation.8 | loop fusion | flops 11534336 | bytes 10485760 | tf_op jit(solution)/shard_map/reduce_sum | solution.py:70
  136.5 0.5 broadcast_multiply_fusion
  137.0 1.0 copy-done.2
  138.1 0.3 copy-done.4
  138.3 2.5 fusion.9
  140.9 8.6 %convolution_convert_fusion = bf16[4096,512]{1,0:T(8,128)(2,1)} fusion(bf16[512,512]{1,0:T(8,128)(2,1)S(1)} %copy-done, f32[4096,512]{1,0:T(8,128)} %copy-done.3, bf16[4096,128]{1,0:T(8,128)(2,1)S(1)} %get-tuple-element.5, bf16[512,128]{1,0:T(8,128)(2,1)S(1)} %copy-done.7, f32[512]{0:T(512)S(1)} %copy-done.8), kind=kOutput, calls=%fused_computation.13 | convolution fusion | flops 2707423232 | bytes 14288896 | tf_op jit(solution)/shard_map/rh,ch->rc/dot_general | solution.py:90
  149.5 4.8 %copy.23 = bf16[2,64,32,512]{3,2,0,1:T(8,128)(2,1)} copy(bf16[2,64,32,512]{3,2,1,0:T(8,128)(2,1)} %bitcast.72) | data formatting | bytes 8388608 | tf_op jit(solution)/shard_map/reshape | solution.py:93
  154.3 5.7 %all-to-all-start.3 = ((bf16[2,64,32,512]{3,2,0,1:T(8,128)(2,1)}), bf16[2,64,32,512]{3,2,0,1:T(8,128)(2,1)}, u32[]{:S(2)}, u32[]{:S(2)}) async-start(bf16[2,64,32,512]{3,2,0,1:T(8,128)(2,1)} %copy.23), calls=%async_computation.3 | async-start | bytes 8388608 | tf_op jit(solution)/shard_map/all_to_all | solution.py:94
  159.9 3.1 %psum.28 = f32[]{:T(128)} all-reduce(f32[]{:T(128)} %get-tuple-element.4), channel_id=1, replica_groups=mesh['member'=2,'grid_0'=4,'grid_1'=4,'grid_2'=4] {'member'}, use_global_device_ids=true, to_apply=%region_6.7 | all-reduce | flops 1 | bytes 8 | tf_op jit(solution)/shard_map/psum | solution.py:24
  163.0 24.4 %psum.29 = f32[]{:T(128)} all-reduce(f32[]{:T(128)} %psum.28), channel_id=1, replica_groups=mesh['member'=2,'grid_0'=4,'grid_1'=4,'grid_2'=4] {'grid_0'}, use_global_device_ids=true, to_apply=%region_7.8 | all-reduce | flops 1 | bytes 8 | tf_op jit(solution)/shard_map/psum | solution.py:24
  187.3 34.6 %psum.30 = f32[]{:T(128)} all-reduce(f32[]{:T(128)} %psum.29), channel_id=1, replica_groups=mesh['member'=2,'grid_0'=4,'grid_1'=4,'grid_2'=4] {'grid_1'}, use_global_device_ids=true, to_apply=%region_8.9 | all-reduce | flops 1 | bytes 8 | tf_op jit(solution)/shard_map/psum | solution.py:24
  222.6 9.3 %psum.31 = f32[]{:T(128)} all-reduce(f32[]{:T(128)} %psum.30), channel_id=1, replica_groups=mesh['member'=2,'grid_0'=4,'grid_1'=4,'grid_2'=4] {'grid_2'}, use_global_device_ids=true, to_apply=%region_9.10 | all-reduce | flops 1 | bytes 8 | tf_op jit(solution)/shard_map/psum | solution.py:24
  232.6 9.8 %convert_bitcast_fusion = bf16[2,64,128,512]{2,3,0,1:T(8,128)(2,1)} fusion(bf16[2,64,32,512]{3,2,0,1:T(8,128)(2,1)} %all-to-all-done.3, bf16[64,32,128]{2,1,0:T(8,128)(2,1)S(1)} %all-to-all-done.1), kind=kOutput, calls=%fused_computation.3 | convolution fusion | flops 545259520 | bytes 21495808 | tf_op jit(solution)/shard_map/dkp,mdkc->mdpc/dot_general | solution.py:95
  242.4 23.4 %copy.24 = bf16[2,64,128,512]{3,1,2,0:T(8,128)(2,1)} copy(bf16[2,64,128,512]{2,3,0,1:T(8,128)(2,1)} %convert_bitcast_fusion) | data formatting | bytes 33554432 | tf_op jit(solution)/shard_map/convert_element_type | solution.py:97
  265.8 7.0 %convolution_bitcast_fusion = f32[2,16,128,512]{3,1,2,0:T(8,128)S(1)} fusion(bf16[2,64,128,512]{3,1,2,0:T(8,128)(2,1)} %copy.24, s32[64]{0:T(128)S(1)} %bitcast.77), kind=kOutput, calls=%fused_computation.16 | convolution fusion | flops 268436480 | bytes 25166080 | tf_op jit(solution)/shard_map/mdpc,db->mbpc/dot_general | solution.py:98
  272.8 8.3 %copy.25 = f32[2,16,128,512]{3,2,1,0:T(8,128)} copy(f32[2,16,128,512]{3,1,2,0:T(8,128)S(1)} %convolution_bitcast_fusion) | data formatting | bytes 16777216 | tf_op jit(solution)/shard_map/mdpc,db->mbpc/transpose | solution.py:98
  (29 shorter events, 0.5 us)
Async XLA Ops:
  7.2 96.4 %copy-start = (bf16[512,512]{1,0:T(8,128)(2,1)S(1)}, bf16[512,512]{1,0:T(8,128)(2,1)}, u32[]{:S(2)}) copy-start(bf16[512,512]{1,0:T(8,128)(2,1)} %param.14) | copy-start | bytes 1572868
  10.8 24.9 %all-to-all-start.1 = ((bf16[64,32,128]{2,1,0:T(8,128)(2,1)}), bf16[64,32,128]{2,1,0:T(8,128)(2,1)S(1)}, u32[]{:S(2)}, u32[]{:S(2)}) async-start(bf16[64,32,128]{2,1,0:T(8,128)(2,1)} %fusion.13), calls=%async_computation.1 | async-start | bytes 1048576 | tf_op jit(solution)/shard_map/all_to_all | solution.py:53
  22.3 106.7 %all-gather.2.cloned.1.call-start = ((), (), s32[]{:S(2)}) async-start(), calls=%async_computation.4 | async-start | bytes 6291456 | tf_op jit(solution)/shard_map/all_gather | solution.py:63
  103.5 2.5 copy-start.7
  103.5 2.5 copy-start.8
  103.6 2.5 copy-start.9
  106.0 4.1 %copy-start.3 = (f32[4096,512]{1,0:T(8,128)}, f32[4096,512]{1,0:T(8,128)S(1)}, u32[]{:S(2)}) copy-start(f32[4096,512]{1,0:T(8,128)S(1)} %fusion.25) | copy-start | bytes 25165828
  106.0 4.1 %copy-start.5 = (s32[1,64]{1,0:T(1,128)S(1)}, s32[1,64]{1,0:T(1,128)}, u32[]{:S(2)}) copy-start(s32[1,64]{1,0:T(1,128)} %param.13) | copy-start | bytes 772
  112.1 15.4 %all-to-all-start = ((f32[64,1,1]{2,1,0:T(1,128)}), f32[64,1,1]{2,1,0:T(1,128)S(1)}, u32[]{:S(2)}, u32[]{:S(2)}) async-start(f32[64,1,1]{2,1,0:T(1,128)} %broadcast_in_dim.2), calls=%async_computation | async-start | bytes 65536 | tf_op jit(solution)/shard_map/all_to_all | solution.py:14
  136.5 1.6 copy-start.2
  136.5 1.8 copy-start.4
  154.3 78.3 %all-to-all-start.3 = ((bf16[2,64,32,512]{3,2,0,1:T(8,128)(2,1)}), bf16[2,64,32,512]{3,2,0,1:T(8,128)(2,1)}, u32[]{:S(2)}, u32[]{:S(2)}) async-start(bf16[2,64,32,512]{3,2,0,1:T(8,128)(2,1)} %copy.23), calls=%async_computation.3 | async-start | bytes 8388608 | tf_op jit(solution)/shard_map/all_to_all | solution.py:94
  242.4 23.4 %copy-start.6 = (s32[1,64]{1,0:T(1,128)S(1)}, s32[1,64]{1,0:T(1,128)}, u32[]{:S(2)}) copy-start(s32[1,64]{1,0:T(1,128)} %param.10) | copy-start | bytes 772
  272.8 8.3 %copy-start.1 = (bf16[512,512]{1,0:T(8,128)(2,1)S(1)}, bf16[512,512]{1,0:T(8,128)(2,1)}, u32[]{:S(2)}) copy-start(bf16[512,512]{1,0:T(8,128)(2,1)} %param.14) | copy-start | bytes 1572868
Sparse Core Ops, SparseCore 0:
  110.3 13.1 all-gather.1
where the time goes:
time: 290 us; the launch traced here: 289 us
  blocking collectives  130 us (45%)
  local copies, waits for them, and re-layouts  49.6 us (17%)
  matrix products  39.9 us (14%)
  starting transfers between devices  23.2 us (8%)
  between operations  17.4 us (6%)
  other arithmetic  16.2 us (6%)
  waiting for transfers between devices  12.2 us (4%)
    psum x4, blocking collectives, one_axis_at_a_time(): value = lax.psum(value, axis)  71.4 us
    all_to_all x1, blocking collectives, per_device(): lax.all_to_all(owner_interp, GRID, split_axis=1, concat_axis=1, tiled=True)  59.1 us
    convert_element_type x1, local copies, waits for them, and re-layouts, per_device(): returned = jnp.einsum('dkp,mdkc->mdpc', owner_weight, owner_grad, preferr...  23.4 us
    all_to_all x1, starting transfers between devices, per_device(): lax.all_to_all(norm_weight, GRID, split_axis=0, concat_axis=0, tiled=True)  11.5 us
    dot_general x1, matrix products, per_device(): jnp.einsum('dkp,mdkc->mdpc', owner_weight, owner_grad, preferred_element_...  9.75 us
    gather x1, local copies, waits for them, and re-layouts, per_device(): picked = local_blocks[:, picked_ids]  9.73 us
    all_to_all x1, waiting for transfers between devices, sent_to_all(): return lax.all_to_all(copies, axis, split_axis=0, concat_axis=0, tiled=True)  9.24 us
    dot_general x1, matrix products, per_device(): jnp.einsum('rh,ch->rc', grad_act, w_in, preferred_element_type=jnp.float32)  8.6 us
  transfers between devices with their start and end apart: 4, of which 2 were waited for; matrix products, arithmetic and copies ran while one was open for 5% of the time, Pallas kernels for 0%

commit v1 on v0

--- a/solution.py
+++ b/solution.py
@@ -54,7 +54,10 @@
     owner_interp = jnp.einsum(
         "dkp,mdpc->mdkc", owner_weight, picked, preferred_element_type=jnp.float32
     ).astype(jnp.bfloat16)
-    interp = lax.all_to_all(owner_interp, GRID, split_axis=1, concat_axis=1, tiled=True)
+    interp = jnp.concatenate(
+        lax.all_to_all(jnp.stack(jnp.split(owner_interp, lax.axis_size(GRID), axis=1)), GRID, 0, 0),
+        axis=1,
+    )
     flat_rows = interp.reshape(members_here * peer_count * slot_count, feature_width)
     pre_act = jnp.dot(flat_rows, w_in, preferred_element_type=jnp.float32) + b_in
     hidden = jax.nn.silu(pre_act).astype(jnp.bfloat16)

time: 290 us -> 291 us (level)
  no operation moved by 1% of the time
where the time goes in v1:
time: 291 us; the launch traced here: 290 us
  blocking collectives  130 us (45%)
  local copies, waits for them, and re-layouts  50 us (17%)
  matrix products  39.9 us (14%)
  starting transfers between devices  23.2 us (8%)
  between operations  17.9 us (6%)
  other arithmetic  16.2 us (6%)
  waiting for transfers between devices  12.2 us (4%)
    psum x4, blocking collectives, one_axis_at_a_time(): value = lax.psum(value, axis)  71.3 us
    all_to_all x1, blocking collectives, per_device(): lax.all_to_all(jnp.stack(jnp.split(owner_interp, lax.axis_size(GRID), axi...  59.1 us
    convert_element_type x1, local copies, waits for them, and re-layouts, per_device(): returned = jnp.einsum('dkp,mdkc->mdpc', owner_weight, owner_grad, preferr...  23.4 us
    all_to_all x1, starting transfers between devices, per_device(): lax.all_to_all(norm_weight, GRID, split_axis=0, concat_axis=0, tiled=True)  11.5 us
    dot_general x1, matrix products, per_device(): jnp.einsum('dkp,mdkc->mdpc', owner_weight, owner_grad, preferred_element_...  9.75 us
    gather x1, local copies, waits for them, and re-layouts, per_device(): picked = local_blocks[:, picked_ids]  9.73 us
    all_to_all x1, waiting for transfers between devices, sent_to_all(): return lax.all_to_all(copies, axis, split_axis=0, concat_axis=0, tiled=True)  9.24 us
    dot_general x1, matrix products, per_device(): jnp.einsum('rh,ch->rc', grad_act, w_in, preferred_element_type=jnp.float32)  8.61 us
  transfers between devices with their start and end apart: 4, of which 2 were waited for; matrix products, arithmetic and copies ran while one was open for 5% of the time, Pallas kernels for 0%

profile of v1, /device:TPU:0, one launch (start us, length us, event | category | flops | bytes accessed | tf_op | source)
XLA Modules:
  0.0 289.9 jit_solution(12123497535253604441)
XLA Ops:
  7.2 1.4 convert_reduce_fusion
  8.6 2.2 fusion.13
  10.8 11.5 %all-to-all-start.1 = ((bf16[64,32,128]{2,1,0:T(8,128)(2,1)}), bf16[64,32,128]{2,1,0:T(8,128)(2,1)S(1)}, u32[]{:S(2)}, u32[]{:S(2)}) async-start(bf16[64,32,128]{2,1,0:T(8,128)(2,1)} %fusion.13), calls=%async_computation.1 | async-start | bytes 1048576 | tf_op jit(solution)/shard_map/all_to_all | solution.py:53
  22.4 0.7 fusion.22
  23.1 9.7 %gather_fusion = bf16[64,2,128,512]{3,2,1,0:T(8,128)(2,1)} fusion(bf16[2,16,128,512]{3,2,1,0:T(8,128)(2,1)} %bitcast.324, s32[1024]{0:T(1024)S(1)} %pad_clamp_fusion), kind=kCustom, calls=%fused_computation | custom fusion | bytes 33554688 | tf_op jit(solution)/shard_map/gather | solution.py:52
  32.8 2.9 %all-to-all-done.1 = bf16[64,32,128]{2,1,0:T(8,128)(2,1)S(1)} async-done(((bf16[64,32,128]{2,1,0:T(8,128)(2,1)}), bf16[64,32,128]{2,1,0:T(8,128)(2,1)S(1)}, u32[]{:S(2)}, u32[]{:S(2)}) %all-to-all-start.1) | async-done | bytes 524320 | tf_op jit(solution)/shard_map/all_to_all | solution.py:53
  35.7 8.1 %convert_bitcast_fusion.1 = bf16[2,64,32,512]{3,2,0,1:T(8,128)(2,1)S(1)} fusion(bf16[64,2,128,512]{3,2,1,0:T(8,128)(2,1)} %gather_fusion, bf16[64,32,128]{2,1,0:T(8,128)(2,1)S(1)} %all-to-all-done.1), kind=kOutput, calls=%fused_computation.15 | convolution fusion | flops 538968064 | bytes 21495808 | tf_op jit(solution)/shard_map/dkp,mdpc->mdkc/dot_general | solution.py:54
  44.8 59.1 %all_to_all.21 = bf16[64,2,1,32,512]{4,3,1,2,0:T(8,128)(2,1)S(1)} all-to-all(bf16[64,2,1,32,512]{4,3,1,2,0:T(8,128)(2,1)S(1)} %constant_dynamic-update-slice_fusion), channel_id=1, replica_groups=mesh['member'=2,'grid_0'=4,'grid_1'=4,'grid_2'=4] {'grid_0','grid_1','gr..., dimensions={0} | all-to-all | bytes 8388608 | tf_op jit(solution)/shard_map/all_to_all | solution.py:58
  103.9 0.6 copy.22
  104.5 2.4 fusion.25
  107.0 4.1 %convolution_add_fusion = f32[4096,128]{1,0:T(8,128)} fusion(bf16[512,128]{1,0:T(8,128)(2,1)S(1)} %copy-done.7, f32[4096,512]{1,0:T(8,128)S(1)} %fusion.25, f32[512]{0:T(512)S(1)} %copy-done.8, f32[128]{0:T(128)S(1)} %copy-done.9), kind=kOutput, calls=%fused_computation.14 | convolution fusion | flops 549978112 | bytes 10619392 | tf_op jit(solution)/shard_map/dot_general | solution.py:64
  111.1 0.7 fusion.18
  111.8 1.3 broadcast_in_dim.2
  113.0 6.0 %all-to-all-start = ((f32[64,1,1]{2,1,0:T(1,128)}), f32[64,1,1]{2,1,0:T(1,128)S(1)}, u32[]{:S(2)}, u32[]{:S(2)}) async-start(f32[64,1,1]{2,1,0:T(1,128)} %broadcast_in_dim.2), calls=%async_computation | async-start | bytes 65536 | tf_op jit(solution)/shard_map/all_to_all | solution.py:14
  119.2 9.2 %all-to-all-done = f32[64,1,1]{2,1,0:T(1,128)S(1)} async-done(((f32[64,1,1]{2,1,0:T(1,128)}), f32[64,1,1]{2,1,0:T(1,128)S(1)}, u32[]{:S(2)}, u32[]{:S(2)}) %all-to-all-start) | async-done | bytes 288 | tf_op jit(solution)/shard_map/all_to_all | solution.py:14
  128.5 0.7 reduce_sum.55
  130.0 7.4 %fusion.4 = (f32[2,64,32,128]{3,2,1,0:T(8,128)S(1)}, f32[2,64,32,128]{3,2,1,0:T(8,128)S(1)}) fusion(f32[4,64,32,128]{3,2,1,0:T(8,128)} %all-gather.2.cloned.1.call-done, f32[2,64,32,128]{3,2,1,0:T(8,128)} %bitcast.326), kind=kLoop, calls=%fused_computation.8 | loop fusion | flops 11534336 | bytes 10485760 | tf_op jit(solution)/shard_map/reduce_sum | solution.py:73
  137.5 0.5 broadcast_multiply_fusion
  138.0 1.0 copy-done.2
  139.0 0.3 copy-done.4
  139.3 2.5 fusion.9
  141.8 8.6 %convolution_convert_fusion = bf16[4096,512]{1,0:T(8,128)(2,1)} fusion(bf16[512,512]{1,0:T(8,128)(2,1)S(1)} %copy-done, f32[4096,512]{1,0:T(8,128)} %copy-done.3, bf16[4096,128]{1,0:T(8,128)(2,1)S(1)} %get-tuple-element.5, bf16[512,128]{1,0:T(8,128)(2,1)S(1)} %copy-done.7, f32[512]{0:T(512)S(1)} %copy-done.8), kind=kOutput, calls=%fused_computation.13 | convolution fusion | flops 2707423232 | bytes 14288896 | tf_op jit(solution)/shard_map/rh,ch->rc/dot_general | solution.py:93
  150.4 4.8 %copy.23 = bf16[2,64,32,512]{3,2,0,1:T(8,128)(2,1)} copy(bf16[2,64,32,512]{3,2,1,0:T(8,128)(2,1)} %bitcast.330) | data formatting | bytes 8388608 | tf_op jit(solution)/shard_map/reshape | solution.py:96
  155.2 5.7 %all-to-all-start.3 = ((bf16[2,64,32,512]{3,2,0,1:T(8,128)(2,1)}), bf16[2,64,32,512]{3,2,0,1:T(8,128)(2,1)}, u32[]{:S(2)}, u32[]{:S(2)}) async-start(bf16[2,64,32,512]{3,2,0,1:T(8,128)(2,1)} %copy.23), calls=%async_computation.3 | async-start | bytes 8388608 | tf_op jit(solution)/shard_map/all_to_all | solution.py:97
  160.9 3.1 %psum.28 = f32[]{:T(128)} all-reduce(f32[]{:T(128)} %get-tuple-element.4), channel_id=1, replica_groups=mesh['member'=2,'grid_0'=4,'grid_1'=4,'grid_2'=4] {'member'}, use_global_device_ids=true, to_apply=%region_6.7 | all-reduce | flops 1 | bytes 8 | tf_op jit(solution)/shard_map/psum | solution.py:24
  163.9 24.3 %psum.29 = f32[]{:T(128)} all-reduce(f32[]{:T(128)} %psum.28), channel_id=1, replica_groups=mesh['member'=2,'grid_0'=4,'grid_1'=4,'grid_2'=4] {'grid_0'}, use_global_device_ids=true, to_apply=%region_7.8 | all-reduce | flops 1 | bytes 8 | tf_op jit(solution)/shard_map/psum | solution.py:24
  188.3 35.0 %psum.30 = f32[]{:T(128)} all-reduce(f32[]{:T(128)} %psum.29), channel_id=1, replica_groups=mesh['member'=2,'grid_0'=4,'grid_1'=4,'grid_2'=4] {'grid_1'}, use_global_device_ids=true, to_apply=%region_8.9 | all-reduce | flops 1 | bytes 8 | tf_op jit(solution)/shard_map/psum | solution.py:24
  223.9 8.9 %psum.31 = f32[]{:T(128)} all-reduce(f32[]{:T(128)} %psum.30), channel_id=1, replica_groups=mesh['member'=2,'grid_0'=4,'grid_1'=4,'grid_2'=4] {'grid_2'}, use_global_device_ids=true, to_apply=%region_9.10 | all-reduce | flops 1 | bytes 8 | tf_op jit(solution)/shard_map/psum | solution.py:24
  233.5 9.8 %convert_bitcast_fusion = bf16[2,64,128,512]{2,3,0,1:T(8,128)(2,1)} fusion(bf16[2,64,32,512]{3,2,0,1:T(8,128)(2,1)} %all-to-all-done.3, bf16[64,32,128]{2,1,0:T(8,128)(2,1)S(1)} %all-to-all-done.1), kind=kOutput, calls=%fused_computation.3 | convolution fusion | flops 545259520 | bytes 21495808 | tf_op jit(solution)/shard_map/dkp,mdkc->mdpc/dot_general | solution.py:98
  243.2 23.4 %copy.24 = bf16[2,64,128,512]{3,1,2,0:T(8,128)(2,1)} copy(bf16[2,64,128,512]{2,3,0,1:T(8,128)(2,1)} %convert_bitcast_fusion) | data formatting | bytes 33554432 | tf_op jit(solution)/shard_map/convert_element_type | solution.py:100
  266.7 7.0 %convolution_bitcast_fusion = f32[2,16,128,512]{3,1,2,0:T(8,128)S(1)} fusion(bf16[2,64,128,512]{3,1,2,0:T(8,128)(2,1)} %copy.24, s32[64]{0:T(128)S(1)} %bitcast.335), kind=kOutput, calls=%fused_computation.16 | convolution fusion | flops 268436480 | bytes 25166080 | tf_op jit(solution)/shard_map/mdpc,db->mbpc/dot_general | solution.py:101
  273.7 8.3 %copy.25 = f32[2,16,128,512]{3,2,1,0:T(8,128)} copy(f32[2,16,128,512]{3,1,2,0:T(8,128)S(1)} %convolution_bitcast_fusion) | data formatting | bytes 16777216 | tf_op jit(solution)/shard_map/mdpc,db->mbpc/transpose | solution.py:101
  (93 shorter events, 0.9 us)
Async XLA Ops:
  7.2 97.3 %copy-start = (bf16[512,512]{1,0:T(8,128)(2,1)S(1)}, bf16[512,512]{1,0:T(8,128)(2,1)}, u32[]{:S(2)}) copy-start(bf16[512,512]{1,0:T(8,128)(2,1)} %param.14) | copy-start | bytes 1572868
  10.8 24.9 %all-to-all-start.1 = ((bf16[64,32,128]{2,1,0:T(8,128)(2,1)}), bf16[64,32,128]{2,1,0:T(8,128)(2,1)S(1)}, u32[]{:S(2)}, u32[]{:S(2)}) async-start(bf16[64,32,128]{2,1,0:T(8,128)(2,1)} %fusion.13), calls=%async_computation.1 | async-start | bytes 1048576 | tf_op jit(solution)/shard_map/all_to_all | solution.py:53
  22.3 107.7 %all-gather.2.cloned.1.call-start = ((), (), s32[]{:S(2)}) async-start(), calls=%async_computation.4 | async-start | bytes 6291456 | tf_op jit(solution)/shard_map/all_gather | solution.py:66
  104.5 2.5 copy-start.7
  104.5 2.5 copy-start.8
  104.5 2.5 copy-start.9
  107.0 4.1 %copy-start.3 = (f32[4096,512]{1,0:T(8,128)}, f32[4096,512]{1,0:T(8,128)S(1)}, u32[]{:S(2)}) copy-start(f32[4096,512]{1,0:T(8,128)S(1)} %fusion.25) | copy-start | bytes 25165828
  107.0 4.1 %copy-start.5 = (s32[1,64]{1,0:T(1,128)S(1)}, s32[1,64]{1,0:T(1,128)}, u32[]{:S(2)}) copy-start(s32[1,64]{1,0:T(1,128)} %param.13) | copy-start | bytes 772
  113.0 15.4 %all-to-all-start = ((f32[64,1,1]{2,1,0:T(1,128)}), f32[64,1,1]{2,1,0:T(1,128)S(1)}, u32[]{:S(2)}, u32[]{:S(2)}) async-start(f32[64,1,1]{2,1,0:T(1,128)} %broadcast_in_dim.2), calls=%async_computation | async-start | bytes 65536 | tf_op jit(solution)/shard_map/all_to_all | solution.py:14
  137.4 1.6 copy-start.2
  137.4 1.8 copy-start.4
  155.2 78.2 %all-to-all-start.3 = ((bf16[2,64,32,512]{3,2,0,1:T(8,128)(2,1)}), bf16[2,64,32,512]{3,2,0,1:T(8,128)(2,1)}, u32[]{:S(2)}, u32[]{:S(2)}) async-start(bf16[2,64,32,512]{3,2,0,1:T(8,128)(2,1)} %copy.23), calls=%async_computation.3 | async-start | bytes 8388608 | tf_op jit(solution)/shard_map/all_to_all | solution.py:97
  243.2 23.4 %copy-start.6 = (s32[1,64]{1,0:T(1,128)S(1)}, s32[1,64]{1,0:T(1,128)}, u32[]{:S(2)}) copy-start(s32[1,64]{1,0:T(1,128)} %param.10) | copy-start | bytes 772
  273.6 8.3 %copy-start.1 = (bf16[512,512]{1,0:T(8,128)(2,1)S(1)}, bf16[512,512]{1,0:T(8,128)(2,1)}, u32[]{:S(2)}) copy-start(bf16[512,512]{1,0:T(8,128)(2,1)} %param.14) | copy-start | bytes 1572868
Sparse Core Ops, SparseCore 0:
  111.2 13.1 all-gather.1
